TPU v7x, 32 devices: a whole 2x2x4 slice. The times are simulated.
32 devices in a mesh: fsdp: 16 (over z, y, x), replica: 2 (over core).
Axes of the slice: x: 2, y: 2, z: 4, core: 2. Of those that a mesh axis runs over, the one named last changes fastest.
Arguments:
- gradients: float32 [2, 4194304], P('replica', 'fsdp'), may hold values from -200 to 200, as said below
- tensor_sizes: int32 [192], replicated, may hold values from 1 to 262144, 4194304 in all
- params: float32 [4194304], P(('fsdp', 'replica')), may hold values from -6 to 6
- first_moment: float32 [4194304], P(('fsdp', 'replica')), may hold values from -6e-06 to 6e-06
- second_moment: float32 [4194304], P(('fsdp', 'replica')), may hold values from 1e-12 to 1e-10
Outputs:
- new_params: float32 [4194304], P(('fsdp', 'replica'))
- new_first: float32 [4194304], P(('fsdp', 'replica'))
- new_second: float32 [4194304], P(('fsdp', 'replica'))
- applied_update: float32 [4194304], P(('fsdp', 'replica'))
Inputs may be any that keep to these rules, and one draw needn't show every extreme that they name: `gradients`: every entry lies within -200 to 200, blocks of 131072 positions having different scales.
All inputs are finite; a program needn't handle non-finite values.
Results may differ from a plain program's by a relative error of at most 0.0055.
Values sent between devices are 32-bit elements.
A program may use at most 64 MiB of HBM per device.

v0:
```python
import math

import jax
import jax.numpy as jnp
from jax import lax
from jax.sharding import PartitionSpec as P


def member_block(tensor_starts, tensor_ends, first_pos, count):
    positions = first_pos + jnp.arange(count, dtype=jnp.int32)
    inside = (positions[:, None] >= tensor_starts[None, :]) & (
        positions[:, None] < tensor_ends[None, :]
    )
    return inside.astype(jnp.float32)


def tensor_sums(values, tensor_starts, tensor_ends, offset_base, block):
    blocks = values.reshape(-1, block)
    tensors = tensor_ends.shape[0]

    def step(total, pair):
        index, rows = pair
        member = member_block(tensor_starts, tensor_ends, offset_base + index * block, block)
        part_sum = jnp.dot(
            rows, member, precision=lax.Precision.HIGHEST, preferred_element_type=jnp.float32
        )
        return (total + part_sum, None)

    counter = jnp.arange(blocks.shape[0], dtype=jnp.int32)
    total, unused = lax.scan(step, jnp.zeros((tensors,), jnp.float32), (counter, blocks))
    return total


def spread_trust(trust, tensor_starts, tensor_ends, offset_base, block, shard_len):

    def step(carry, index):
        member = member_block(tensor_starts, tensor_ends, offset_base + index * block, block)
        return (
            carry,
            jnp.dot(
                member, trust, precision=lax.Precision.HIGHEST, preferred_element_type=jnp.float32
            ),
        )

    counter = jnp.arange(shard_len // block, dtype=jnp.int32)
    unused, rows = lax.scan(step, 0, counter)
    return rows.reshape(shard_len)


def shards(gradients, tensor_sizes, params, first_moment, second_moment):
    reduced = lax.psum_scatter(gradients, "replica", scatter_dimension=1, tiled=True)[0]
    grad = reduced / lax.axis_size("replica")
    shard_len = params.shape[0]
    block = math.gcd(shard_len, 4096)
    offset_base = lax.axis_index(("fsdp", "replica")) * shard_len
    tensor_ends = jnp.cumsum(tensor_sizes, dtype=jnp.int32)
    tensor_starts = tensor_ends - tensor_sizes
    local_sq = jnp.sum(grad * grad)
    param_part = tensor_sums(params * params, tensor_starts, tensor_ends, offset_base, block)
    grad_sq = lax.psum(local_sq, ("fsdp", "replica"))
    param_sq = lax.psum(param_part, ("fsdp", "replica"))
    clip_scale = jnp.minimum(1.0, 1.0 / jnp.sqrt(grad_sq))
    clipped = clip_scale * grad
    new_first = 0.9 * first_moment + 0.1 * clipped
    new_second = 0.999 * second_moment + 0.001 * clipped * clipped
    direction = (
        new_first / (1.0 - 0.9**20) / (jnp.sqrt(new_second / (1.0 - 0.999**20)) + 1e-08)
        + 0.01 * params
    )
    update_part = tensor_sums(direction * direction, tensor_starts, tensor_ends, offset_base, block)
    paired = lax.psum(update_part, "replica")
    update_sq = lax.psum(paired, "fsdp")
    both_pos = (param_sq > 0) & (update_sq > 0)
    trust = jnp.where(
        both_pos, jnp.sqrt(param_sq) / jnp.sqrt(jnp.where(both_pos, update_sq, 1.0)), 1.0
    )
    trust_rows = spread_trust(trust, tensor_starts, tensor_ends, offset_base, block, shard_len)
    applied_update = trust_rows * direction
    new_params = params - 0.01 * applied_update
    return (new_params, new_first, new_second, applied_update)


def solution(mesh):
    placed = (
        P("replica", "fsdp"),
        P(),
        P(("fsdp", "replica")),
        P(("fsdp", "replica")),
        P(("fsdp", "replica")),
    )
    return jax.shard_map(
        shards,
        mesh=mesh,
        in_specs=placed,
        out_specs=(
            P(("fsdp", "replica")),
            P(("fsdp", "replica")),
            P(("fsdp", "replica")),
            P(("fsdp", "replica")),
        ),
        check_vma=False,
    )
```

profile of v0, /device:TPU:0, one launch (start us, length us, event | category | flops | bytes accessed | tf_op | source)
XLA Modules:
  0.0 429.8 jit_solution(14212660780549110103)
XLA Ops:
  8.8 93.3 %while.33 = (s32[]{:T(128)}, f32[192]{0:T(256)S(1)}, f32[32,4096]{1,0:T(8,128)S(1)}, s32[32]{0:T(128)S(1)}, s32[]{:T(128)}, /*index=5*/s32[192]{0:T(256)S(1)}, s32[192]{0:T(256)S(1)}, s32[]{:T(128)}, s32[1]{0:T(128)}, s32[]{:T(128)}) while((s32[]{:T(128)}, f32[192]{0:T(256)S(1)}, f32[32,4096]{1,0:T(8,128)S(1)}, s32[32]{0:T(128)S(1)}, ...), condition=%wide.region_3.4_spmd.clone, body=%wide.region_2.3_spmd.clone.sunk | while | flops 11800965 | bytes 54427 | solution.py:30
  103.4 2.7 multiply_reduce_fusion
  106.1 42.1 %all-reduce.2 = (f32[]{:T(128)}, f32[192]{0:T(256)S(1)}) all-reduce(f32[]{:T(128)} %multiply_reduce_fusion, f32[192]{0:T(256)S(1)} %get-tuple-element.115), channel_id=1, replica_groups=mesh['fsdp'=16,'replica'=2] {'fsdp','replica'}, use_global_device_ids=true, to_apply=%region_7.8 | all-reduce | flops 193 | bytes 1544 | tf_op jit(solution)/shard_map/psum | solution.py:60
  150.9 97.2 %while.34 = (s32[]{:T(128)}, f32[192]{0:T(256)S(1)}, f32[32,4096]{1,0:T(8,128)S(1)}, s32[32]{0:T(128)S(1)}, s32[]{:T(128)}, /*index=5*/s32[192]{0:T(256)S(1)}, s32[192]{0:T(256)S(1)}, s32[]{:T(128)}, s32[1]{0:T(128)}, s32[]{:T(128)}) while((s32[]{:T(128)}, f32[192]{0:T(256)S(1)}, f32[32,4096]{1,0:T(8,128)S(1)}, s32[32]{0:T(128)S(1)}, ...), condition=%wide.region_9.10_spmd.clone, body=%wide.region_8.9_spmd.clone.sunk | while | flops 11800965 | bytes 54427 | solution.py:30
  248.1 2.5 psum.30
  250.6 40.7 %psum.31 = f32[192]{0:T(256)S(1)} all-reduce(f32[192]{0:T(256)S(1)} %psum.30), channel_id=1, replica_groups=mesh['fsdp'=16,'replica'=2] {'fsdp'}, use_global_device_ids=true, to_apply=%region_11.12 | all-reduce | flops 192 | bytes 1536 | tf_op jit(solution)/shard_map/psum | solution.py:72
  291.3 130.2 %while.32 = (s32[]{:T(128)}, f32[32,4096]{1,0:T(8,128)S(1)}, s32[32]{0:T(128)S(1)}, s32[]{:T(128)}, s32[192]{0:T(256)S(1)}, /*index=5*/s32[192]{0:T(256)S(1)}, f32[192]{0:T(256)S(1)}, s32[]{:T(128)}, s32[1]{0:T(128)}, s32[]{:T(128)}) while((s32[]{:T(128)}, f32[32,4096]{1,0:T(8,128)S(1)}, s32[32]{0:T(128)S(1)}, s32[]{:T(128)}, ...), condition=%wide.region_13.14_spmd, body=%wide.region_12.13_spmd.sunk | while | flops 11800580 | bytes 84369 | solution.py:46
  292.6 2.4 fusion.32
  296.7 2.4 fusion.32
  300.7 2.4 fusion.32
  304.8 2.4 fusion.32
  308.9 2.4 fusion.32
  312.9 2.4 fusion.32
  317.0 2.4 fusion.32
  321.1 2.4 fusion.32
  325.1 2.4 fusion.32
  329.2 2.4 fusion.32
  333.3 2.4 fusion.32
  337.3 2.4 fusion.32
  386.2 2.4 fusion.32
  390.2 2.4 fusion.32
  394.3 2.4 fusion.32
  398.4 2.4 fusion.32
  402.4 2.4 fusion.32
  (408 shorter events, 218.1 us)
Async XLA Ops:
  7.2 0.8 copy-start.6
  7.2 1.4 copy-start
  7.2 96.2 %all-reduce.5.cloned.1.call-start = ((), (), s32[]{:S(2)}) async-start(), calls=%async_computation | async-start | bytes 2097152
  8.8 93.3 %copy-start.7 = (u32[32]{0:T(128)S(1)}, u32[32]{0:T(128)}, u32[]{:S(2)}) copy-start(u32[32]{0:T(128)} %constant.78) | copy-start | bytes 388
  102.0 48.3 %copy-start.3 = (f32[131072]{0:T(1024)S(1)}, f32[131072]{0:T(1024)}, u32[]{:S(2)}) copy-start(f32[131072]{0:T(1024)} %param.14) | copy-start | bytes 1572868
  102.1 48.3 %copy-start.4 = (f32[131072]{0:T(1024)S(1)}, f32[131072]{0:T(1024)}, u32[]{:S(2)}) copy-start(f32[131072]{0:T(1024)} %param.15) | copy-start | bytes 1572868
  150.8 270.9 %copy-start.1 = (f32[131072]{0:T(1024)}, f32[131072]{0:T(1024)S(1)}, u32[]{:S(2)}) copy-start(f32[131072]{0:T(1024)S(1)} %get-tuple-element.213) | copy-start | bytes 1572868
  150.8 270.9 %copy-start.2 = (f32[131072]{0:T(1024)}, f32[131072]{0:T(1024)S(1)}, u32[]{:S(2)}) copy-start(f32[131072]{0:T(1024)S(1)} %get-tuple-element.214) | copy-start | bytes 1572868
  150.9 140.4 %copy-start.5 = (f32[32,4096]{1,0:T(8,128)S(1)}, f32[32,4096]{1,0:T(8,128)}, u32[]{:S(2)}) copy-start(f32[32,4096]{1,0:T(8,128)} %custom-call.2) | copy-start | bytes 1572868
Sparse Core Ops, SparseCore 0:
  10.3 22.1 all-reduce.4
where the time goes:
time: 431 us; the launch traced here: 430 us
  matrix products  181 us (42%)
  blocking collectives  85.3 us (20%)
  local copies, waits for them, and re-layouts  72.1 us (17%)
  loops' own time  67 us (16%)
  between operations  15.6 us (4%)
  other arithmetic  7.62 us (2%)
    dot_general x64, matrix products, step(): jnp.dot(rows, member, precision=lax.Precision.HIGHEST, preferred_element_...  104 us
    dot_general x32, matrix products, step(): jnp.dot(member, trust, precision=lax.Precision.HIGHEST, preferred_element...  77.2 us
    dynamic_slice x96, local copies, waits for them, and re-layouts, tensor_sums(): lax.scan(step, jnp.zeros((tensors,), jnp.float32), (counter, blocks))  58.8 us
    another operation x2, loops' own time, tensor_sums(): lax.scan(step, jnp.zeros((tensors,), jnp.float32), (counter, blocks))  45 us
    psum x1, blocking collectives, shards(): grad_sq = lax.psum(local_sq, ('fsdp', 'replica'))  42.1 us
    psum x1, blocking collectives, shards(): update_sq = lax.psum(paired, 'fsdp')  40.7 us
    another operation x1, loops' own time, spread_trust(): unused, rows = lax.scan(step, 0, counter)  21.9 us
    dynamic_update_slice x32, local copies, waits for them, and re-layouts, spread_trust(): unused, rows = lax.scan(step, 0, counter)  12.1 us
  transfers between devices with their start and end apart: 1, of which 0 were waited for; matrix products, arithmetic and copies ran while one was open for 17% of the time, Pallas kernels for 0%

commit v1 on v0

v1 whole, which is shorter than its diff:
```python
import functools

import jax
import jax.numpy as jnp
from jax import lax
from jax.experimental import pallas as pl
from jax.experimental.pallas import tpu as pltpu
from jax.sharding import PartitionSpec as P

MESH = pl.DeviceIdType.MESH
LANES = 128
F32 = jnp.float32
BF16 = jnp.bfloat16


def round_up(value, unit):
    return -(-value // unit) * unit


def in_hbm(value):
    return pltpu.with_memory_space_constraint(value, pltpu.HBM)


def split(value):
    high = value.astype(BF16)
    return high, (value - high.astype(F32)).astype(BF16)


def running_ends(sizes_row, tcol, trow):
    low = (sizes_row & 4095).astype(F32)
    high = (sizes_row >> 12).astype(F32)
    sub = lax.broadcasted_iota(jnp.int32, (trow, trow), 0)
    lane = lax.broadcasted_iota(jnp.int32, (trow, trow), 1)

    def column(part):
        return jnp.sum(jnp.where(lane <= sub, part, 0.0), axis=1, keepdims=True)

    def row(part):
        own = jnp.sum(jnp.where(lane == sub, part, 0.0), axis=1, keepdims=True)
        return jnp.sum(jnp.where(sub <= lane, own, 0.0), axis=0, keepdims=True)

    def joined(form):
        return form(low).astype(jnp.int32) + (form(high).astype(jnp.int32) << 12)

    size_col = joined(
        lambda part: jnp.sum(jnp.where(lane == sub, part, 0.0), axis=1, keepdims=True)
    )
    return joined(column)[:tcol], size_col[:tcol], joined(row)


def lamb_kernel(
    fsdp, replica, sizes_ref, grads_ref, params_ref, first_ref, second_ref,
    nf_ref, ns_ref, dir_ref, par_ref, mt_ref, w_ref,
    sizes_pad, own_half, peer_half, got_half, mom1, mom2, mask, parts,
    gather_g, gather_p, gather_u, load_sem, half_send, half_recv, send_sem, recv_sem,
):
    n = fsdp * replica
    rows = par_ref.shape[0]
    tcol = mask.shape[0] // 3
    trow = mt_ref.shape[1] // 3
    f_me = lax.axis_index("fsdp")
    r_me = lax.axis_index("replica")
    me = f_me * replica + r_me
    base = me * (rows * LANES)

    def place(k):
        peer = lax.rem(me + k, n)
        return (lax.div(peer, replica), lax.rem(peer, replica))

    def half(c):
        return grads_ref.at[pl.ds(pl.multiple_of(c * rows, rows), rows)]

    peer_loads = []
    for k in range(1, replica):
        peer_loads.append(
            pltpu.make_async_copy(half(lax.rem(r_me + k, replica)), peer_half.at[k - 1], load_sem.at[4 + k])
        )
    for copy in peer_loads:
        copy.start()
    own_load = pltpu.make_async_copy(half(r_me), own_half, load_sem.at[0])
    par_load = pltpu.make_async_copy(params_ref, par_ref, load_sem.at[1])
    mom1_load = pltpu.make_async_copy(first_ref, mom1, load_sem.at[2])
    mom2_load = pltpu.make_async_copy(second_ref, mom2, load_sem.at[3])
    for copy in (par_load, own_load, mom1_load, mom2_load):
        copy.start()

    barrier = pltpu.get_barrier_semaphore()

    def greet(k, carry):
        pl.semaphore_signal(barrier, inc=1, device_id=place(k), device_id_type=MESH)
        return carry

    lax.fori_loop(1, n, greet, 0)

    sizes_pad[...] = jnp.zeros_like(sizes_pad)
    sizes_pad[:, : sizes_ref.shape[1]] = sizes_ref[...]
    end_col, size_col, end_row = running_ends(sizes_pad[...], tcol, trow)
    sizes_row = sizes_pad[...]
    extent = rows * LANES

    def local(pos):
        return jnp.clip(pos - base, 0, extent)

    sc, ec = local(end_col - size_col), local(end_col)
    sr, er = local(end_row - sizes_row), local(end_row)
    sc_row, ec_row = sc >> 7, ec >> 7
    sr_row, er_row = sr >> 7, er >> 7
    lane = lax.broadcasted_iota(jnp.int32, (tcol, LANES), 1)
    after = lane >= (sc & 127)
    before = lane < (ec & 127)
    same = sc_row == ec_row
    start_w = jnp.where(after & (before | jnp.logical_not(same)), 1.0, 0.0)
    end_w = jnp.where(before & jnp.logical_not(same), 1.0, 0.0)

    def as_mask(cond):
        return jnp.where(cond, 1.0, 0.0).astype(BF16)

    step = 256
    for at in range(0, rows, step):
        r = at + lax.broadcasted_iota(jnp.int32, (tcol, step), 1)
        mask[0:tcol, at : at + step] = as_mask((r > sc_row) & (r < ec_row))
        mask[tcol : 2 * tcol, at : at + step] = as_mask(r == sc_row)
        mask[2 * tcol : 3 * tcol, at : at + step] = as_mask(r == ec_row)

    eye = lax.broadcasted_iota(jnp.int32, (tcol, trow), 0) == lax.broadcasted_iota(
        jnp.int32, (tcol, trow), 1
    )

    def sums_row():
        y = jnp.dot(mask[...], parts[...], preferred_element_type=F32)
        y = y[:, :LANES] + y[:, LANES:]
        total = y[0:tcol] + y[tcol : 2 * tcol] * start_w + y[2 * tcol : 3 * tcol] * end_w
        col = jnp.sum(total, axis=1, keepdims=True)
        return jnp.sum(jnp.where(eye, col, 0.0), axis=0, keepdims=True)

    for copy in peer_loads:
        copy.wait()
    pl.semaphore_wait(barrier, n - 1)

    swaps = []
    for k in range(1, replica):
        swaps.append(
            pltpu.make_async_remote_copy(
                src_ref=peer_half.at[k - 1],
                dst_ref=got_half.at[k - 1],
                send_sem=half_send.at[k - 1],
                recv_sem=half_recv.at[k - 1],
                device_id=(f_me, lax.rem(r_me + k, replica)),
                device_id_type=MESH,
            )
        )
    for copy in swaps:
        copy.start()

    par_load.wait()
    block = 128
    for at in range(0, rows, block):
        p = par_ref[at : at + block]
        high, low = split(p * p)
        parts[at : at + block, :LANES] = high
        parts[at : at + block, LANES:] = low
    gather_p[me] = sums_row()

    def share(buffer, which):
        def send(k, carry):
            pltpu.make_async_remote_copy(
                src_ref=buffer.at[me],
                dst_ref=buffer.at[me],
                send_sem=send_sem.at[which],
                recv_sem=recv_sem.at[which],
                device_id=place(k),
                device_id_type=MESH,
            ).start()
            return carry

        lax.fori_loop(1, n, send, 0)

    def arrive(buffer, which):
        most = buffer.at[pl.ds(0, n - 1)]
        pltpu.make_async_copy(most, most, recv_sem.at[which]).wait()

    def leave(buffer, which):
        most = buffer.at[pl.ds(0, n - 1)]
        pltpu.make_async_copy(most, most, send_sem.at[which]).wait()

    own_load.wait()
    for copy in swaps:
        copy.wait()
    acc = jnp.zeros((8, LANES), F32)
    for at in range(0, rows, block):
        g = own_half[at : at + block]
        for k in range(replica - 1):
            g = g + got_half[k, at : at + block]
        g = g * (1.0 / replica)
        own_half[at : at + block] = g
        acc = acc + jnp.sum((g * g).reshape(block // 8, 8, LANES), axis=0)
    gather_g[me] = jnp.sum(acc, axis=0, keepdims=True)
    share(gather_g, 0)
    share(gather_p, 1)

    for at in range(0, rows, block):
        r = at + lax.broadcasted_iota(jnp.int32, (block, trow), 0)
        mt_ref[at : at + block, 0:trow] = as_mask((r > sr_row) & (r < er_row))
        mt_ref[at : at + block, trow : 2 * trow] = as_mask(r == sr_row)
        mt_ref[at : at + block, 2 * trow : 3 * trow] = as_mask(r == er_row)
    w_ref[...] = jnp.zeros_like(w_ref)

    mom1_load.wait()
    mom2_load.wait()
    arrive(gather_g, 0)
    grad_sq = jnp.sum(jnp.sum(gather_g[...], axis=0), axis=1, keepdims=True)
    clip = jnp.minimum(1.0, 1.0 / jnp.sqrt(grad_sq))
    c1 = 1.0 - 0.9**20
    c2 = 1.0 / (1.0 - 0.999**20)
    for at in range(0, rows, block):
        clipped = own_half[at : at + block] * clip
        nf = 0.9 * mom1[at : at + block] + 0.1 * clipped
        ns = 0.999 * mom2[at : at + block] + 0.001 * clipped * clipped
        nf_ref[at : at + block] = nf
        ns_ref[at : at + block] = ns
        d = nf / (c1 * (jnp.sqrt(ns * c2) + 1e-08)) + 0.01 * par_ref[at : at + block]
        dir_ref[at : at + block] = d
        high, low = split(d * d)
        parts[at : at + block, :LANES] = high
        parts[at : at + block, LANES:] = low
    gather_u[me] = sums_row()
    share(gather_u, 2)
    arrive(gather_p, 1)
    param_sq = jnp.sum(gather_p[...], axis=0)
    arrive(gather_u, 2)
    update_sq = jnp.sum(gather_u[...], axis=0)
    both = (param_sq > 0) & (update_sq > 0)
    trust_row = jnp.where(both, jnp.sqrt(param_sq) / jnp.sqrt(jnp.where(both, update_sq, 1.0)), 1.0)
    trust = jnp.sum(jnp.where(eye, trust_row, 0.0), axis=1, keepdims=True)
    weights = (jnp.broadcast_to(trust, (tcol, LANES)), trust * start_w, trust * end_w)
    for slot, weight in enumerate(weights):
        high, low = split(weight)
        w_ref[slot * trow : slot * trow + tcol, :LANES] = high
        w_ref[slot * trow : slot * trow + tcol, LANES:] = low
    leave(gather_g, 0)
    leave(gather_p, 1)
    leave(gather_u, 2)


def apply_kernel(nf_ref, ns_ref, dir_ref, par_ref, mt_ref, w_ref, np_out, nf_out, ns_out, ap_out,
                 np_buf, ap_buf, sem, chunk_sem):
    rows = dir_ref.shape[0]
    early = [
        pltpu.make_async_copy(nf_ref, nf_out, sem.at[0]),
        pltpu.make_async_copy(ns_ref, ns_out, sem.at[1]),
    ]
    for copy in early:
        copy.start()
    chunks = chunk_sem.shape[1]
    block = rows // chunks
    late = []
    for i in range(chunks):
        part = pl.ds(i * block, block)
        t = jnp.dot(mt_ref[part], w_ref[...], preferred_element_type=F32)
        applied = (t[:, :LANES] + t[:, LANES:]) * dir_ref[part]
        ap_buf[part] = applied
        np_buf[part] = par_ref[part] - 0.01 * applied
        for j, (src, dst) in enumerate(((ap_buf, ap_out), (np_buf, np_out))):
            copy = pltpu.make_async_copy(src.at[part], dst.at[part], chunk_sem.at[j, i])
            copy.start()
            late.append(copy)
    for copy in early + late:
        copy.wait()


def shards(fsdp, replica, gradients, tensor_sizes, params, first_moment, second_moment):
    n = fsdp * replica
    rows = params.shape[0] // LANES
    tcol = round_up(tensor_sizes.shape[0], 16)
    trow = round_up(tensor_sizes.shape[0], LANES)
    hbm = pl.BlockSpec(memory_space=pltpu.HBM)
    vmem = pl.BlockSpec(memory_space=pltpu.VMEM)
    flat = (rows, LANES)
    mids = pl.pallas_call(
        functools.partial(lamb_kernel, fsdp, replica),
        out_shape=[
            pltpu.VMEM(flat, F32),
            pltpu.VMEM(flat, F32),
            pltpu.VMEM(flat, F32),
            pltpu.VMEM(flat, F32),
            pltpu.VMEM((rows, 3 * trow), BF16),
            pltpu.VMEM((3 * trow, 2 * LANES), BF16),
        ],
        in_specs=[vmem, hbm, hbm, hbm, hbm],
        out_specs=[vmem] * 6,
        scratch_shapes=[
            pltpu.VMEM((1, trow), jnp.int32),
            pltpu.VMEM(flat, F32),
            pltpu.VMEM((replica - 1,) + flat, F32),
            pltpu.VMEM((replica - 1,) + flat, F32),
            pltpu.VMEM(flat, F32),
            pltpu.VMEM(flat, F32),
            pltpu.VMEM((3 * tcol, rows), BF16),
            pltpu.VMEM((rows, 2 * LANES), BF16),
            pltpu.VMEM((n, 1, LANES), F32),
            pltpu.VMEM((n, 1, trow), F32),
            pltpu.VMEM((n, 1, trow), F32),
            pltpu.SemaphoreType.DMA((4 + replica,)),
            pltpu.SemaphoreType.DMA((replica - 1,)),
            pltpu.SemaphoreType.DMA((replica - 1,)),
            pltpu.SemaphoreType.DMA((3,)),
            pltpu.SemaphoreType.DMA((3,)),
        ],
        compiler_params=pltpu.CompilerParams(
            collective_id=0, has_side_effects=True, vmem_limit_bytes=24 * 1024 * 1024
        ),
    )(
        tensor_sizes.reshape(1, -1),
        in_hbm(gradients.reshape(replica * rows, LANES)),
        in_hbm(params.reshape(flat)),
        in_hbm(first_moment.reshape(flat)),
        in_hbm(second_moment.reshape(flat)),
    )
    chunks = 4
    outs = pl.pallas_call(
        apply_kernel,
        out_shape=[jax.ShapeDtypeStruct(flat, F32)] * 4,
        in_specs=[vmem] * 6,
        out_specs=[hbm] * 4,
        scratch_shapes=[
            pltpu.VMEM(flat, F32),
            pltpu.VMEM(flat, F32),
            pltpu.SemaphoreType.DMA((2,)),
            pltpu.SemaphoreType.DMA((2, chunks)),
        ],
        compiler_params=pltpu.CompilerParams(vmem_limit_bytes=24 * 1024 * 1024),
    )(*mids)
    return tuple(out.reshape(-1) for out in outs)


def solution(mesh):
    flat = P(("fsdp", "replica"))
    return jax.shard_map(
        functools.partial(shards, mesh.shape["fsdp"], mesh.shape["replica"]),
        mesh=mesh,
        in_specs=(P("replica", "fsdp"), P(), flat, flat, flat),
        out_specs=(flat,) * 4,
        check_vma=False,
    )
```

time: 431 us -> 22.5 us (0.05)
  matrix products: 181 us -> 0 us
  blocking collectives: 85.3 us -> 0 us
  local copies, waits for them, and re-layouts: 72.1 us -> 0.67 us
  loops' own time: 67 us -> 0 us
  Pallas kernels: 0 us -> 21 us
  between operations: 15.6 us -> 0.65 us
  other arithmetic: 7.62 us -> 0 us
    dot_general x96 -> x0, matrix products: 181 us -> none  [the longest x64 104 us: step(): jnp.dot(rows, member, precision=lax.Precision.HIGHEST, preferred_element_...]
    psum x3 -> x0, blocking collectives: 85.3 us -> none  [the longest x1 42.1 us: shards(): grad_sq = lax.psum(local_sq, ('fsdp', 'replica'))]
    another operation x3 -> x0, loops' own time: 67 us -> none  [the longest x2 45 us: tensor_sums(): lax.scan(step, jnp.zeros((tensors,), jnp.float32), (counter, blocks))]
    dynamic_slice x96 -> x0, local copies, waits for them, and re-layouts: 58.8 us -> none  [tensor_sums(): lax.scan(step, jnp.zeros((tensors,), jnp.float32), (counter, blocks))]
    pallas_call x0 -> x2, Pallas kernels: none -> 21 us  [the longest x1 19.6 us: shards(): pl.pallas_call(functools.partial(lamb_kernel, fsdp, replica), out_shape=[...]
    dynamic_update_slice x32 -> x0, local copies, waits for them, and re-layouts: 12.1 us -> none  [spread_trust(): unused, rows = lax.scan(step, 0, counter)]
  transfers between devices with their start and end apart: 1 -> 0, of which waited for: 0 -> 0; matrix products, arithmetic and copies ran while one was open for 17% -> 0% of each run, Pallas kernels for 0% -> 0%
where the time goes in v1:
time: 22.5 us; the launch traced here: 22.4 us
  Pallas kernels  21 us (93%)
  local copies, waits for them, and re-layouts  0.67 us (3%)
  between operations  0.65 us (3%)
    pallas_call x1, Pallas kernels, shards(): pl.pallas_call(functools.partial(lamb_kernel, fsdp, replica), out_shape=[...  19.6 us
    pallas_call x1, Pallas kernels, shards(): pl.pallas_call(apply_kernel, out_shape=[jax.ShapeDtypeStruct(flat, F32)]...  1.47 us
    unnamed x2, local copies, waits for them, and re-layouts  0.67 us

profile of v1, /device:TPU:0, one launch (start us, length us, event | category | flops | bytes accessed | tf_op | source)
XLA Modules:
  0.0 22.4 jit_solution(13608184918058738685)
XLA Ops:
  0.6 0.0 copy-start
  0.6 0.7 %copy-done = s32[192]{0:T(256)S(1)} copy-done((s32[192]{0:T(256)S(1)}, s32[192]{0:T(256)}, u32[]{:S(2)}) %copy-start) | copy-done | bytes 792
  1.3 19.6 %shard_map.84 = (f32[1024,128]{1,0:T(8,128)S(1)}, f32[1024,128]{1,0:T(8,128)S(1)}, f32[1024,128]{1,0:T(8,128)S(1)}, f32[1024,128]{1,0:T(8,128)S(1)}, bf16[1024,7...) custom-call(s32[1,192]{1,0:T(1,128)S(1)} %bitcast.9, f32[2048,128]{1,0:T(8,128)} %bitcast.10, f32[1024,128]{1,0:T(8,128)} %bitcast.11, ...), custom_call_target="tpu_custom_call" | custom-call | tf_op jit(solution)/shard_map/pallas_call | solution.py:279
  20.9 1.5 %shard_map.85 = (f32[1024,128]{1,0:T(8,128)}, f32[1024,128]{1,0:T(8,128)}, f32[1024,128]{1,0:T(8,128)}, f32[1024,128]{1,0:T(8,128)}) custom-call(f32[1024,128]{1,0:T(8,128)S(1)} %get-tuple-element.14.nf_ref, f32[1024,128]{1,0:T(8,128)S(1)} %get-tuple-element.15.ns_ref, f32[1024,128]{1,0:T(8,128)S(1)} %get-tuple-element.16.dir_ref, ...), custom_call_target="tpu_custom_call" | custom-call | tf_op jit(solution)/shard_map/pallas_call | solution.py:320
Async XLA Ops:
  0.6 0.7 %copy-start = (s32[192]{0:T(256)S(1)}, s32[192]{0:T(256)}, u32[]{:S(2)}) copy-start(s32[192]{0:T(256)} %param.6) | copy-start | bytes 2308

commit v2 on v1

--- a/solution.py
+++ b/solution.py
@@ -51,8 +51,9 @@
 def lamb_kernel(
     fsdp, replica, sizes_ref, grads_ref, params_ref, first_ref, second_ref,
     nf_ref, ns_ref, dir_ref, par_ref, mt_ref, w_ref,
-    sizes_pad, own_half, peer_half, got_half, mom1, mom2, mask, parts,
-    gather_g, gather_p, gather_u, load_sem, half_send, half_recv, send_sem, recv_sem,
+    sizes_in, sizes_pad, own_half, peer_half, got_half, mom1, mom2, mask, parts,
+    gather_g, gather_p, gather_u, load_sem, peer_sem, half_send, half_recv, send_sem, recv_sem,
+    ready_sem, all_sem,
 ):
     n = fsdp * replica
     rows = par_ref.shape[0]
@@ -62,40 +63,121 @@
     r_me = lax.axis_index("replica")
     me = f_me * replica + r_me
     base = me * (rows * LANES)
-
-    def place(k):
-        peer = lax.rem(me + k, n)
-        return (lax.div(peer, replica), lax.rem(peer, replica))
-
-    def half(c):
-        return grads_ref.at[pl.ds(pl.multiple_of(c * rows, rows), rows)]
-
-    peer_loads = []
-    for k in range(1, replica):
-        peer_loads.append(
-            pltpu.make_async_copy(half(lax.rem(r_me + k, replica)), peer_half.at[k - 1], load_sem.at[4 + k])
-        )
-    for copy in peer_loads:
-        copy.start()
-    own_load = pltpu.make_async_copy(half(r_me), own_half, load_sem.at[0])
+    twin = (f_me, 1 - r_me)
+    barrier = pltpu.get_barrier_semaphore()
+
+    def chip(k):
+        f = f_me + k
+        return jnp.where(f >= fsdp, f - fsdp, f)
+
+    @pl.when(r_me == 0)
+    def _():
+        pl.semaphore_signal(barrier, inc=1, device_id=twin, device_id_type=MESH)
+
+    pieces = peer_sem.shape[0]
+    size = rows // pieces
+
+    def piece(c, i):
+        return grads_ref.at[pl.ds(pl.multiple_of(c * rows + i * size, size), size)]
+
+    peer_loads = [
+        pltpu.make_async_copy(piece(1 - r_me, i), peer_half.at[pl.ds(i * size, size)], peer_sem.at[i])
+        for i in range(pieces)
+    ]
+    own_load = pltpu.make_async_copy(
+        grads_ref.at[pl.ds(pl.multiple_of(r_me * rows, rows), rows)], own_half, load_sem.at[0]
+    )
+    sizes_load = pltpu.make_async_copy(sizes_ref, sizes_in, load_sem.at[4])
     par_load = pltpu.make_async_copy(params_ref, par_ref, load_sem.at[1])
     mom1_load = pltpu.make_async_copy(first_ref, mom1, load_sem.at[2])
     mom2_load = pltpu.make_async_copy(second_ref, mom2, load_sem.at[3])
-    for copy in (par_load, own_load, mom1_load, mom2_load):
+    for copy in peer_loads + [own_load, sizes_load, par_load, mom1_load, mom2_load]:
         copy.start()
 
-    barrier = pltpu.get_barrier_semaphore()
-
-    def greet(k, carry):
-        pl.semaphore_signal(barrier, inc=1, device_id=place(k), device_id_type=MESH)
-        return carry
-
-    lax.fori_loop(1, n, greet, 0)
-
+    @pl.when(r_me == 1)
+    def _():
+        pl.semaphore_wait(barrier, 1)
+        pl.semaphore_signal(ready_sem, inc=1, device_id=twin, device_id_type=MESH)
+
+    @pl.when(r_me == 0)
+    def _():
+        pl.semaphore_wait(ready_sem, 1)
+
+        def greet(k, carry):
+            pl.semaphore_signal(barrier, inc=1, device_id=(chip(k), 0), device_id_type=MESH)
+            return carry
+
+        lax.fori_loop(1, fsdp, greet, 0)
+
+    swaps = [
+        pltpu.make_async_remote_copy(
+            src_ref=peer_half.at[pl.ds(i * size, size)],
+            dst_ref=got_half.at[pl.ds(i * size, size)],
+            send_sem=half_send.at[i],
+            recv_sem=half_recv.at[i],
+            device_id=twin,
+            device_id_type=MESH,
+        )
+        for i in range(pieces)
+    ]
+    for load, copy in zip(peer_loads, swaps):
+        load.wait()
+        copy.start()
+
+    def share(buffer, which):
+        def send(place):
+            pltpu.make_async_remote_copy(
+                src_ref=buffer.at[me],
+                dst_ref=buffer.at[me],
+                send_sem=send_sem.at[which],
+                recv_sem=recv_sem.at[which],
+                device_id=place,
+                device_id_type=MESH,
+            ).start()
+
+        def send_chip(k, carry):
+            for c in range(replica):
+                send((chip(k), c))
+            return carry
+
+        lax.fori_loop(1, fsdp, send_chip, 0)
+        send(twin)
+
+    def arrive(buffer, which):
+        most = buffer.at[pl.ds(0, n - 1)]
+        pltpu.make_async_copy(most, most, recv_sem.at[which]).wait()
+
+    def leave(buffer, which):
+        most = buffer.at[pl.ds(0, n - 1)]
+        pltpu.make_async_copy(most, most, send_sem.at[which]).wait()
+
+    block = 128
+    own_load.wait()
+    acc = jnp.zeros((8, LANES), F32)
+    for i in range(pieces):
+        swaps[i].wait_recv()
+        for at in range(i * size, (i + 1) * size, block):
+            g = (own_half[at : at + block] + got_half[at : at + block]) * (1.0 / replica)
+            own_half[at : at + block] = g
+            acc = acc + jnp.sum((g * g).reshape(block // 8, 8, LANES), axis=0)
+    gather_g[me] = jnp.sum(acc, axis=0, keepdims=True)
+
+    @pl.when(r_me == 0)
+    def _():
+        pl.semaphore_wait(barrier, fsdp - 1)
+        pl.semaphore_signal(all_sem, inc=1, device_id=twin, device_id_type=MESH)
+
+    @pl.when(r_me == 1)
+    def _():
+        pl.semaphore_wait(all_sem, 1)
+
+    share(gather_g, 0)
+
+    sizes_load.wait()
     sizes_pad[...] = jnp.zeros_like(sizes_pad)
-    sizes_pad[:, : sizes_ref.shape[1]] = sizes_ref[...]
-    end_col, size_col, end_row = running_ends(sizes_pad[...], tcol, trow)
+    sizes_pad[:, : sizes_in.shape[1]] = sizes_in[...]
     sizes_row = sizes_pad[...]
+    end_col, size_col, end_row = running_ends(sizes_row, tcol, trow)
     extent = rows * LANES
 
     def local(pos):
@@ -133,77 +215,14 @@
         col = jnp.sum(total, axis=1, keepdims=True)
         return jnp.sum(jnp.where(eye, col, 0.0), axis=0, keepdims=True)
 
-    for copy in peer_loads:
-        copy.wait()
-    pl.semaphore_wait(barrier, n - 1)
-
-    swaps = []
-    for k in range(1, replica):
-        swaps.append(
-            pltpu.make_async_remote_copy(
-                src_ref=peer_half.at[k - 1],
-                dst_ref=got_half.at[k - 1],
-                send_sem=half_send.at[k - 1],
-                recv_sem=half_recv.at[k - 1],
-                device_id=(f_me, lax.rem(r_me + k, replica)),
-                device_id_type=MESH,
-            )
-        )
-    for copy in swaps:
-        copy.start()
-
     par_load.wait()
-    block = 128
     for at in range(0, rows, block):
         p = par_ref[at : at + block]
         high, low = split(p * p)
         parts[at : at + block, :LANES] = high
         parts[at : at + block, LANES:] = low
     gather_p[me] = sums_row()
-
-    def share(buffer, which):
-        def send(k, carry):
-            pltpu.make_async_remote_copy(
-                src_ref=buffer.at[me],
-                dst_ref=buffer.at[me],
-                send_sem=send_sem.at[which],
-                recv_sem=recv_sem.at[which],
-                device_id=place(k),
-                device_id_type=MESH,
-            ).start()
-            return carry
-
-        lax.fori_loop(1, n, send, 0)
-
-    def arrive(buffer, which):
-        most = buffer.at[pl.ds(0, n - 1)]
-        pltpu.make_async_copy(most, most, recv_sem.at[which]).wait()
-
-    def leave(buffer, which):
-        most = buffer.at[pl.ds(0, n - 1)]
-        pltpu.make_async_copy(most, most, send_sem.at[which]).wait()
-
-    own_load.wait()
-    for copy in swaps:
-        copy.wait()
-    acc = jnp.zeros((8, LANES), F32)
-    for at in range(0, rows, block):
-        g = own_half[at : at + block]
-        for k in range(replica - 1):
-            g = g + got_half[k, at : at + block]
-        g = g * (1.0 / replica)
-        own_half[at : at + block] = g
-        acc = acc + jnp.sum((g * g).reshape(block // 8, 8, LANES), axis=0)
-    gather_g[me] = jnp.sum(acc, axis=0, keepdims=True)
-    share(gather_g, 0)
     share(gather_p, 1)
-
-    for at in range(0, rows, block):
-        r = at + lax.broadcasted_iota(jnp.int32, (block, trow), 0)
-        mt_ref[at : at + block, 0:trow] = as_mask((r > sr_row) & (r < er_row))
-        mt_ref[at : at + block, trow : 2 * trow] = as_mask(r == sr_row)
-        mt_ref[at : at + block, 2 * trow : 3 * trow] = as_mask(r == er_row)
-    w_ref[...] = jnp.zeros_like(w_ref)
 
     mom1_load.wait()
     mom2_load.wait()
@@ -225,8 +244,20 @@
         parts[at : at + block, LANES:] = low
     gather_u[me] = sums_row()
     share(gather_u, 2)
+
+    for at in range(0, rows, block):
+        r = at + lax.broadcasted_iota(jnp.int32, (block, trow), 0)
+        mt_ref[at : at + block, 0:trow] = as_mask((r > sr_row) & (r < er_row))
+        mt_ref[at : at + block, trow : 2 * trow] = as_mask(r == sr_row)
+        mt_ref[at : at + block, 2 * trow : 3 * trow] = as_mask(r == er_row)
+    w_ref[...] = jnp.zeros_like(w_ref)
+
     arrive(gather_p, 1)
     param_sq = jnp.sum(gather_p[...], axis=0)
+    for copy in swaps:
+        copy.wait_send()
+    leave(gather_g, 0)
+    leave(gather_p, 1)
     arrive(gather_u, 2)
     update_sq = jnp.sum(gather_u[...], axis=0)
     both = (param_sq > 0) & (update_sq > 0)
@@ -237,8 +268,6 @@
         high, low = split(weight)
         w_ref[slot * trow : slot * trow + tcol, :LANES] = high
         w_ref[slot * trow : slot * trow + tcol, LANES:] = low
-    leave(gather_g, 0)
-    leave(gather_p, 1)
     leave(gather_u, 2)
 
 
@@ -269,6 +298,7 @@
 
 
 def shards(fsdp, replica, gradients, tensor_sizes, params, first_moment, second_moment):
+    assert replica == 2
     n = fsdp * replica
     rows = params.shape[0] // LANES
     tcol = round_up(tensor_sizes.shape[0], 16)
@@ -276,6 +306,7 @@
     hbm = pl.BlockSpec(memory_space=pltpu.HBM)
     vmem = pl.BlockSpec(memory_space=pltpu.VMEM)
     flat = (rows, LANES)
+    pieces = 4
     mids = pl.pallas_call(
         functools.partial(lamb_kernel, fsdp, replica),
         out_shape=[
@@ -286,13 +317,14 @@
             pltpu.VMEM((rows, 3 * trow), BF16),
             pltpu.VMEM((3 * trow, 2 * LANES), BF16),
         ],
-        in_specs=[vmem, hbm, hbm, hbm, hbm],
+        in_specs=[hbm] * 5,
         out_specs=[vmem] * 6,
         scratch_shapes=[
+            pltpu.VMEM((1, tensor_sizes.shape[0]), jnp.int32),
             pltpu.VMEM((1, trow), jnp.int32),
             pltpu.VMEM(flat, F32),
-            pltpu.VMEM((replica - 1,) + flat, F32),
-            pltpu.VMEM((replica - 1,) + flat, F32),
+            pltpu.VMEM(flat, F32),
+            pltpu.VMEM(flat, F32),
             pltpu.VMEM(flat, F32),
             pltpu.VMEM(flat, F32),
             pltpu.VMEM((3 * tcol, rows), BF16),
@@ -300,17 +332,20 @@
             pltpu.VMEM((n, 1, LANES), F32),
             pltpu.VMEM((n, 1, trow), F32),
             pltpu.VMEM((n, 1, trow), F32),
-            pltpu.SemaphoreType.DMA((4 + replica,)),
-            pltpu.SemaphoreType.DMA((replica - 1,)),
-            pltpu.SemaphoreType.DMA((replica - 1,)),
+            pltpu.SemaphoreType.DMA((5,)),
+            pltpu.SemaphoreType.DMA((pieces,)),
+            pltpu.SemaphoreType.DMA((pieces,)),
+            pltpu.SemaphoreType.DMA((pieces,)),
             pltpu.SemaphoreType.DMA((3,)),
             pltpu.SemaphoreType.DMA((3,)),
+            pltpu.SemaphoreType.REGULAR,
+            pltpu.SemaphoreType.REGULAR,
         ],
         compiler_params=pltpu.CompilerParams(
             collective_id=0, has_side_effects=True, vmem_limit_bytes=24 * 1024 * 1024
         ),
     )(
-        tensor_sizes.reshape(1, -1),
+        in_hbm(tensor_sizes.reshape(1, -1)),
         in_hbm(gradients.reshape(replica * rows, LANES)),
         in_hbm(params.reshape(flat)),
         in_hbm(first_moment.reshape(flat)),

time: 22.5 us -> 20.6 us (0.916)
  Pallas kernels: 21 us -> 19.8 us
  local copies, waits for them, and re-layouts: 0.67 us -> 0 us
    pallas_call x1, Pallas kernels: 19.6 us -> 18.3 us  [shards(): pl.pallas_call(functools.partial(lamb_kernel, fsdp, replica), out_shape=[...]
    unnamed x2 -> x0, local copies, waits for them, and re-layouts: 0.67 us -> none
where the time goes in v2:
time: 20.6 us; the launch traced here: 20.4 us
  Pallas kernels  19.8 us (96%)
  between operations  0.64 us (3%)
    pallas_call x1, Pallas kernels, shards(): pl.pallas_call(functools.partial(lamb_kernel, fsdp, replica), out_shape=[...  18.3 us
    pallas_call x1, Pallas kernels, shards(): pl.pallas_call(apply_kernel, out_shape=[jax.ShapeDtypeStruct(flat, F32)]...  1.47 us

profile of v2, /device:TPU:0, one launch (start us, length us, event | category | flops | bytes accessed | tf_op | source)
XLA Modules:
  0.0 20.4 jit_solution(861516290381092864)
XLA Ops:
  0.6 18.3 %shard_map.84 = (f32[1024,128]{1,0:T(8,128)S(1)}, f32[1024,128]{1,0:T(8,128)S(1)}, f32[1024,128]{1,0:T(8,128)S(1)}, f32[1024,128]{1,0:T(8,128)S(1)}, bf16[1024,7...) custom-call(s32[1,192]{1,0:T(1,128)} %bitcast.13, f32[2048,128]{1,0:T(8,128)} %bitcast.9, f32[1024,128]{1,0:T(8,128)} %bitcast.10, ...), custom_call_target="tpu_custom_call" | custom-call | tf_op jit(solution)/shard_map/pallas_call | solution.py:310
  19.0 1.5 %shard_map.85 = (f32[1024,128]{1,0:T(8,128)}, f32[1024,128]{1,0:T(8,128)}, f32[1024,128]{1,0:T(8,128)}, f32[1024,128]{1,0:T(8,128)}) custom-call(f32[1024,128]{1,0:T(8,128)S(1)} %get-tuple-element.14.nf_ref, f32[1024,128]{1,0:T(8,128)S(1)} %get-tuple-element.15.ns_ref, f32[1024,128]{1,0:T(8,128)S(1)} %get-tuple-element.16.dir_ref, ...), custom_call_target="tpu_custom_call" | custom-call | tf_op jit(solution)/shard_map/pallas_call | solution.py:355

commit v3 on v2

--- a/solution.py
+++ b/solution.py
@@ -53,7 +53,7 @@
     nf_ref, ns_ref, dir_ref, par_ref, mt_ref, w_ref,
     sizes_in, sizes_pad, own_half, peer_half, got_half, mom1, mom2, mask, parts,
     gather_g, gather_p, gather_u, load_sem, peer_sem, half_send, half_recv, send_sem, recv_sem,
-    ready_sem, all_sem,
+    near_send, near_recv, ready_sem, all_sem,
 ):
     n = fsdp * replica
     rows = par_ref.shape[0]
@@ -124,13 +124,13 @@
         load.wait()
         copy.start()
 
-    def share(buffer, which):
+    def share(buffer):
         def send(place):
             pltpu.make_async_remote_copy(
                 src_ref=buffer.at[me],
                 dst_ref=buffer.at[me],
-                send_sem=send_sem.at[which],
-                recv_sem=recv_sem.at[which],
+                send_sem=send_sem,
+                recv_sem=recv_sem,
                 device_id=place,
                 device_id_type=MESH,
             ).start()
@@ -143,13 +143,50 @@
         lax.fori_loop(1, fsdp, send_chip, 0)
         send(twin)
 
-    def arrive(buffer, which):
+    def finish(buffer, sem):
         most = buffer.at[pl.ds(0, n - 1)]
-        pltpu.make_async_copy(most, most, recv_sem.at[which]).wait()
-
-    def leave(buffer, which):
-        most = buffer.at[pl.ds(0, n - 1)]
-        pltpu.make_async_copy(most, most, send_sem.at[which]).wait()
+        pltpu.make_async_copy(most, most, sem).wait()
+
+    reach = gather_p.shape[0] // 2
+    offsets = [o for o in range(-reach, reach + 1) if o != 0]
+
+    def within(pos):
+        return (pos >= 0) & (pos < n)
+
+    def near_copy(buffer, which, o):
+        to = jnp.clip(me + o, 0, n - 1)
+        return pltpu.make_async_remote_copy(
+            src_ref=buffer.at[reach],
+            dst_ref=buffer.at[reach - o],
+            send_sem=near_send.at[which, o + reach],
+            recv_sem=near_recv.at[which, o + reach],
+            device_id=(lax.div(to, replica), lax.rem(to, replica)),
+            device_id_type=MESH,
+        )
+
+    def near_start(buffer, which):
+        for o in sorted(offsets, key=abs, reverse=True):
+            @pl.when(within(me + o))
+            def _():
+                near_copy(buffer, which, o).start()
+
+    def near_clear(buffer):
+        for o in offsets:
+            @pl.when(jnp.logical_not(within(me - o)))
+            def _():
+                buffer[reach - o] = jnp.zeros(buffer.shape[1:], F32)
+
+    def near_arrive(buffer, which):
+        for o in offsets:
+            @pl.when(within(me - o))
+            def _():
+                near_copy(buffer, which, o).wait_recv()
+
+    def near_leave(buffer, which):
+        for o in offsets:
+            @pl.when(within(me + o))
+            def _():
+                near_copy(buffer, which, o).wait_send()
 
     block = 128
     own_load.wait()
@@ -171,7 +208,9 @@
     def _():
         pl.semaphore_wait(all_sem, 1)
 
-    share(gather_g, 0)
+    share(gather_g)
+    near_clear(gather_p)
+    near_clear(gather_u)
 
     sizes_load.wait()
     sizes_pad[...] = jnp.zeros_like(sizes_pad)
@@ -221,12 +260,12 @@
         high, low = split(p * p)
         parts[at : at + block, :LANES] = high
         parts[at : at + block, LANES:] = low
-    gather_p[me] = sums_row()
-    share(gather_p, 1)
+    gather_p[reach] = sums_row()
+    near_start(gather_p, 0)
 
     mom1_load.wait()
     mom2_load.wait()
-    arrive(gather_g, 0)
+    finish(gather_g, recv_sem)
     grad_sq = jnp.sum(jnp.sum(gather_g[...], axis=0), axis=1, keepdims=True)
     clip = jnp.minimum(1.0, 1.0 / jnp.sqrt(grad_sq))
     c1 = 1.0 - 0.9**20
@@ -242,8 +281,8 @@
         high, low = split(d * d)
         parts[at : at + block, :LANES] = high
         parts[at : at + block, LANES:] = low
-    gather_u[me] = sums_row()
-    share(gather_u, 2)
+    gather_u[reach] = sums_row()
+    near_start(gather_u, 1)
 
     for at in range(0, rows, block):
         r = at + lax.broadcasted_iota(jnp.int32, (block, trow), 0)
@@ -252,13 +291,13 @@
         mt_ref[at : at + block, 2 * trow : 3 * trow] = as_mask(r == er_row)
     w_ref[...] = jnp.zeros_like(w_ref)
 
-    arrive(gather_p, 1)
+    near_arrive(gather_p, 0)
     param_sq = jnp.sum(gather_p[...], axis=0)
     for copy in swaps:
         copy.wait_send()
-    leave(gather_g, 0)
-    leave(gather_p, 1)
-    arrive(gather_u, 2)
+    finish(gather_g, send_sem)
+    near_leave(gather_p, 0)
+    near_arrive(gather_u, 1)
     update_sq = jnp.sum(gather_u[...], axis=0)
     both = (param_sq > 0) & (update_sq > 0)
     trust_row = jnp.where(both, jnp.sqrt(param_sq) / jnp.sqrt(jnp.where(both, update_sq, 1.0)), 1.0)
@@ -268,7 +307,7 @@
         high, low = split(weight)
         w_ref[slot * trow : slot * trow + tcol, :LANES] = high
         w_ref[slot * trow : slot * trow + tcol, LANES:] = low
-    leave(gather_u, 2)
+    near_leave(gather_u, 1)
 
 
 def apply_kernel(nf_ref, ns_ref, dir_ref, par_ref, mt_ref, w_ref, np_out, nf_out, ns_out, ap_out,
@@ -307,6 +346,7 @@
     vmem = pl.BlockSpec(memory_space=pltpu.VMEM)
     flat = (rows, LANES)
     pieces = 4
+    reach = -(-n // 16)
     mids = pl.pallas_call(
         functools.partial(lamb_kernel, fsdp, replica),
         out_shape=[
@@ -330,14 +370,16 @@
             pltpu.VMEM((3 * tcol, rows), BF16),
             pltpu.VMEM((rows, 2 * LANES), BF16),
             pltpu.VMEM((n, 1, LANES), F32),
-            pltpu.VMEM((n, 1, trow), F32),
-            pltpu.VMEM((n, 1, trow), F32),
+            pltpu.VMEM((2 * reach + 1, 1, trow), F32),
+            pltpu.VMEM((2 * reach + 1, 1, trow), F32),
             pltpu.SemaphoreType.DMA((5,)),
             pltpu.SemaphoreType.DMA((pieces,)),
             pltpu.SemaphoreType.DMA((pieces,)),
             pltpu.SemaphoreType.DMA((pieces,)),
-            pltpu.SemaphoreType.DMA((3,)),
-            pltpu.SemaphoreType.DMA((3,)),
+            pltpu.SemaphoreType.DMA,
+            pltpu.SemaphoreType.DMA,
+            pltpu.SemaphoreType.DMA((2, 2 * reach + 1)),
+            pltpu.SemaphoreType.DMA((2, 2 * reach + 1)),
             pltpu.SemaphoreType.REGULAR,
             pltpu.SemaphoreType.REGULAR,
         ],

time: 20.6 us -> 17.1 us (0.83)
  Pallas kernels: 19.8 us -> 16.3 us
    pallas_call x1, Pallas kernels: 18.3 us -> 14.8 us  [shards(): pl.pallas_call(functools.partial(lamb_kernel, fsdp, replica), out_shape=[...]
where the time goes in v3:
time: 17.1 us; the launch traced here: 17 us
  Pallas kernels  16.3 us (95%)
  between operations  0.64 us (4%)
    pallas_call x1, Pallas kernels, shards(): pl.pallas_call(functools.partial(lamb_kernel, fsdp, replica), out_shape=[...  14.8 us
    pallas_call x1, Pallas kernels, shards(): pl.pallas_call(apply_kernel, out_shape=[jax.ShapeDtypeStruct(flat, F32)]...  1.47 us

profile of v3, /device:TPU:0, one launch (start us, length us, event | category | flops | bytes accessed | tf_op | source)
XLA Modules:
  0.0 17.0 jit_solution(6854457357572837893)
XLA Ops:
  0.6 14.8 %shard_map.84 = (f32[1024,128]{1,0:T(8,128)S(1)}, f32[1024,128]{1,0:T(8,128)S(1)}, f32[1024,128]{1,0:T(8,128)S(1)}, f32[1024,128]{1,0:T(8,128)S(1)}, bf16[1024,7...) custom-call(s32[1,192]{1,0:T(1,128)} %bitcast.13, f32[2048,128]{1,0:T(8,128)} %bitcast.9, f32[1024,128]{1,0:T(8,128)} %bitcast.10, ...), custom_call_target="tpu_custom_call" | custom-call | tf_op jit(solution)/shard_map/pallas_call | solution.py:350
  15.5 1.5 %shard_map.85 = (f32[1024,128]{1,0:T(8,128)}, f32[1024,128]{1,0:T(8,128)}, f32[1024,128]{1,0:T(8,128)}, f32[1024,128]{1,0:T(8,128)}) custom-call(f32[1024,128]{1,0:T(8,128)S(1)} %get-tuple-element.14.nf_ref, f32[1024,128]{1,0:T(8,128)S(1)} %get-tuple-element.15.ns_ref, f32[1024,128]{1,0:T(8,128)S(1)} %get-tuple-element.16.dir_ref, ...), custom_call_target="tpu_custom_call" | custom-call | tf_op jit(solution)/shard_map/pallas_call | solution.py:397

commit v4 on v3

--- a/solution.py
+++ b/solution.py
@@ -188,6 +188,11 @@
             def _():
                 near_copy(buffer, which, o).wait_send()
 
+    @pl.when(r_me == 0)
+    def _():
+        pl.semaphore_wait(barrier, fsdp - 1)
+        pl.semaphore_signal(all_sem, inc=1, device_id=twin, device_id_type=MESH)
+
     block = 128
     own_load.wait()
     acc = jnp.zeros((8, LANES), F32)
@@ -199,11 +204,6 @@
             acc = acc + jnp.sum((g * g).reshape(block // 8, 8, LANES), axis=0)
     gather_g[me] = jnp.sum(acc, axis=0, keepdims=True)
 
-    @pl.when(r_me == 0)
-    def _():
-        pl.semaphore_wait(barrier, fsdp - 1)
-        pl.semaphore_signal(all_sem, inc=1, device_id=twin, device_id_type=MESH)
-
     @pl.when(r_me == 1)
     def _():
         pl.semaphore_wait(all_sem, 1)
@@ -247,9 +247,11 @@
         jnp.int32, (tcol, trow), 1
     )
 
-    def sums_row():
-        y = jnp.dot(mask[...], parts[...], preferred_element_type=F32)
-        y = y[:, :LANES] + y[:, LANES:]
+    def masked(at, span):
+        y = jnp.dot(mask[:, at : at + span], parts[at : at + span], preferred_element_type=F32)
+        return y[:, :LANES] + y[:, LANES:]
+
+    def sums_row(y):
         total = y[0:tcol] + y[tcol : 2 * tcol] * start_w + y[2 * tcol : 3 * tcol] * end_w
         col = jnp.sum(total, axis=1, keepdims=True)
         return jnp.sum(jnp.where(eye, col, 0.0), axis=0, keepdims=True)
@@ -260,28 +262,41 @@
         high, low = split(p * p)
         parts[at : at + block, :LANES] = high
         parts[at : at + block, LANES:] = low
-    gather_p[reach] = sums_row()
+    gather_p[reach] = sums_row(masked(0, rows))
     near_start(gather_p, 0)
 
     mom1_load.wait()
     mom2_load.wait()
+    for at in range(0, rows, block):
+        g = own_half[at : at + block]
+        mom1[at : at + block] = 0.9 * mom1[at : at + block]
+        mom2[at : at + block] = 0.999 * mom2[at : at + block]
+        got_half[at : at + block] = 0.001 * (g * g)
     finish(gather_g, recv_sem)
     grad_sq = jnp.sum(jnp.sum(gather_g[...], axis=0), axis=1, keepdims=True)
     clip = jnp.minimum(1.0, 1.0 / jnp.sqrt(grad_sq))
     c1 = 1.0 - 0.9**20
     c2 = 1.0 / (1.0 - 0.999**20)
-    for at in range(0, rows, block):
-        clipped = own_half[at : at + block] * clip
-        nf = 0.9 * mom1[at : at + block] + 0.1 * clipped
-        ns = 0.999 * mom2[at : at + block] + 0.001 * clipped * clipped
-        nf_ref[at : at + block] = nf
-        ns_ref[at : at + block] = ns
-        d = nf / (c1 * (jnp.sqrt(ns * c2) + 1e-08)) + 0.01 * par_ref[at : at + block]
-        dir_ref[at : at + block] = d
-        high, low = split(d * d)
-        parts[at : at + block, :LANES] = high
-        parts[at : at + block, LANES:] = low
-    gather_u[reach] = sums_row()
+    tenth, clip_sq = 0.1 * clip, clip * clip
+    halves = 2
+    span = rows // halves
+    y = None
+    for h in range(halves):
+        for at in range(h * span, (h + 1) * span, block):
+            nf = mom1[at : at + block] + tenth * own_half[at : at + block]
+            ns = mom2[at : at + block] + clip_sq * got_half[at : at + block]
+            nf_ref[at : at + block] = nf
+            ns_ref[at : at + block] = ns
+            root = ns * c2
+            root = root * lax.rsqrt(root)
+            d = nf / (c1 * root + c1 * 1e-08) + 0.01 * par_ref[at : at + block]
+            dir_ref[at : at + block] = d
+            high, low = split(d * d)
+            parts[at : at + block, :LANES] = high
+            parts[at : at + block, LANES:] = low
+        part = masked(h * span, span)
+        y = part if y is None else y + part
+    gather_u[reach] = sums_row(y)
     near_start(gather_u, 1)
 
     for at in range(0, rows, block):

time: 17.1 us -> 17.1 us (level)
  no operation moved by 1% of the time
where the time goes in v4:
time: 17.1 us; the launch traced here: 17 us
  Pallas kernels  16.4 us (96%)
  between operations  0.64 us (4%)
    pallas_call x1, Pallas kernels, shards(): pl.pallas_call(functools.partial(lamb_kernel, fsdp, replica), out_shape=[...  14.9 us
    pallas_call x1, Pallas kernels, shards(): pl.pallas_call(apply_kernel, out_shape=[jax.ShapeDtypeStruct(flat, F32)]...  1.47 us

profile of v4, /device:TPU:0, one launch (start us, length us, event | category | flops | bytes accessed | tf_op | source)
XLA Modules:
  0.0 17.0 jit_solution(1728482600573185970)
XLA Ops:
  0.6 14.9 %shard_map.84 = (f32[1024,128]{1,0:T(8,128)S(1)}, f32[1024,128]{1,0:T(8,128)S(1)}, f32[1024,128]{1,0:T(8,128)S(1)}, f32[1024,128]{1,0:T(8,128)S(1)}, bf16[1024,7...) custom-call(s32[1,192]{1,0:T(1,128)} %bitcast.13, f32[2048,128]{1,0:T(8,128)} %bitcast.9, f32[1024,128]{1,0:T(8,128)} %bitcast.10, ...), custom_call_target="tpu_custom_call" | custom-call | tf_op jit(solution)/shard_map/pallas_call | solution.py:365
  15.5 1.5 %shard_map.85 = (f32[1024,128]{1,0:T(8,128)}, f32[1024,128]{1,0:T(8,128)}, f32[1024,128]{1,0:T(8,128)}, f32[1024,128]{1,0:T(8,128)}) custom-call(f32[1024,128]{1,0:T(8,128)S(1)} %get-tuple-element.14.nf_ref, f32[1024,128]{1,0:T(8,128)S(1)} %get-tuple-element.15.ns_ref, f32[1024,128]{1,0:T(8,128)S(1)} %get-tuple-element.16.dir_ref, ...), custom_call_target="tpu_custom_call" | custom-call | tf_op jit(solution)/shard_map/pallas_call | solution.py:412
